TPU v7x, 256 devices: a whole 4x4x8 slice. The times are simulated.
256 devices in a mesh: gx: 64 (over x, z_hi, y, core), gy: 4 (over z_lo).
Axes of the slice: x: 4, y: 4, z: 8 (z_hi: 2, z_lo: 4; z = z_hi * 4 + z_lo), core: 2. Of those that a mesh axis runs over, the one named last changes fastest.
Arguments:
- adjoint: float32 [9, 256, 128, 512], P(None, 'gx', 'gy'), may hold values from -6 to 6
- buoyancy: float32 [256, 128, 512], P('gx', 'gy'), may hold values from 0.5 to 2
- lame_lambda: float32 [256, 128, 512], P('gx', 'gy'), may hold values from 0.5 to 2
- shear_mu: float32 [256, 128, 512], P('gx', 'gy'), may hold values from 0.3 to 1.2
- packed: int32 [64, 64, 4, 12, 256], P('gx', None, 'gy'), may hold values from -2147483648 to 2147483646
- scales: float32 [64, 64, 4, 12], P('gx', None, 'gy'), may hold values from 0.005 to 0.05
- perm: int32 [64, 64], P('gx'), may hold values from 0 to 63, each once within a row
Outputs:
- adjoint_out: float32 [9, 256, 128, 512], P(None, 'gx', 'gy')
- gradients: float32 [2, 256, 128, 512], P(None, 'gx', 'gy')
Inputs may be any that keep to these rules, and one draw needn't show every extreme that they name: Each row of perm names every number 0 to 63 once. The words of packed are stored inputs and may cross devices as they are, four signed bytes to a word; only values that a program computes travel in float32.
All inputs are finite; a program needn't handle non-finite values.
Results may differ from a plain program's by a relative error of at most 0.0003.
Values sent between devices are 32-bit elements; how exact they have to be, the bound alone decides.
A program may use at most 128 MiB of HBM per device.

v0:
```python
import functools

import jax
import jax.numpy as jnp
from jax import lax
from jax.experimental import pallas as pl
from jax.experimental.pallas import tpu as pltpu
from jax.sharding import PartitionSpec as P

MESH = pl.DeviceIdType.MESH
STEPS = 2
COURANT = 0.15
ROWS = 8
PIECES = 2

VX, VY, VZ, SXX, SYY, SZZ, SXY, SXZ, SYZ = range(9)

STRESS_X = ((0, (SXX,), -1), (1, (SXY, SXZ), 1))
STRESS_Y = ((0, (SYY,), -1), (1, (SXY, SYZ), 1))
SPEED_X = ((3, (VY, VZ), -1), (5, (VX,), 1))
SPEED_Y = ((3, (VX, VZ), -1), (5, (VY,), 1))


def partner(me, distance, count):
    if count & (count - 1):
        return lax.rem(me + distance, count)
    result, bit = me, 1
    while bit < count:
        if distance & bit:
            result = result + bit - 2 * bit * ((me // bit) % 2)
        bit *= 2
    return result


def kernel(n_x, n_y, adj, buoy, lam, shear, packed, scales, perm, out, grads,
           cur, coef, strain, halo_x, halo_y, send_y, factors, factor_s, inv,
           in_sem, xs_sem, xr_sem, ys_sem, yr_sem, ws_sem, wr_sem, fs_sem, fr_sem, loc_sem, *words):
    cx, cy, cz = buoy.shape
    comp = packed.shape[1]
    per_step = comp // STEPS
    lanes = packed.shape[3]
    segw = packed.shape[2] * lanes
    tiles = cy // ROWS
    pieces = xs_sem.shape[1]
    part = cy // pieces
    me_x, me_y = lax.axis_index("gx"), lax.axis_index("gy")

    loads = []
    for index in (SXX, SXY, SXZ, SYY, SYZ, SZZ, VX, VY, VZ):
        loads.append(pltpu.make_async_copy(adj.at[index], cur.at[index, pl.ds(1, cx)], in_sem.at[index]))
    for index, ref in enumerate((buoy, lam, shear)):
        loads.append(pltpu.make_async_copy(ref, coef.at[index], in_sem.at[9 + index]))
    own_words = [pltpu.make_async_copy(packed.at[me_x, pl.ds(step * per_step, per_step)], words[step].at[me_x],
                                       loc_sem.at[2 + step]) for step in range(STEPS)]
    own_factor = pltpu.make_async_copy(scales.at[0, me_x], factors.at[me_x], loc_sem.at[1])
    for copy in loads:
        copy.start()
    for copy in own_words:
        copy.start()
    own_factor.start()

    barrier = pltpu.get_barrier_semaphore()
    for distance in range(1, n_x):
        pl.semaphore_signal(barrier, inc=1, device_id={"gx": partner(me_x, distance, n_x)}, device_id_type=MESH)

    def edge(way, axis):
        me, count = (me_x, n_x) if axis == "gx" else (me_y, n_y)
        return (me > 0) if way < 0 else (me < count - 1)

    for way in (-1, 1):
        @pl.when(edge(way, "gy"))
        def _():
            pl.semaphore_signal(barrier, inc=1, device_id={"gy": me_y + way}, device_id_type=MESH)

    pl.semaphore_wait(barrier, n_x - 1 + jnp.minimum(me_y, 1) + jnp.minimum(n_y - 1 - me_y, 1))

    def copy_x(step, message, source, piece):
        start, fields, way = message
        slot = 6 * step + start
        return pltpu.make_async_remote_copy(
            src_ref=source(fields, way, piece),
            dst_ref=halo_x.at[pl.ds(slot, len(fields)), pl.ds(piece * part, part)],
            send_sem=xs_sem.at[slot, piece], recv_sem=xr_sem.at[slot, piece],
            device_id={"gx": me_x + way}, device_id_type=MESH)

    def copy_y(step, message):
        start, fields, way = message
        slot = 6 * step + start
        return pltpu.make_async_remote_copy(
            src_ref=send_y.at[pl.ds(slot, len(fields))], dst_ref=halo_y.at[pl.ds(slot, len(fields))],
            send_sem=ys_sem.at[slot], recv_sem=yr_sem.at[slot],
            device_id={"gy": me_y + way}, device_id_type=MESH)

    def layer(fields, way, piece):
        return cur.at[pl.ds(fields[0], len(fields)), 1 if way < 0 else cx, pl.ds(piece * part, part)]

    def first_layer(fields, way, piece):
        return adj.at[pl.ds(fields[0], len(fields)), 0 if way < 0 else cx - 1, pl.ds(piece * part, part)]

    def word_copy(distance, step):
        to = partner(me_x, distance, n_x)
        stored = pl.ds(step * per_step, per_step)
        return pltpu.make_async_remote_copy(
            src_ref=packed.at[to, stored], dst_ref=words[step].at[me_x], send_sem=ws_sem.at[distance, step],
            recv_sem=wr_sem.at[distance, step], device_id={"gx": to}, device_id_type=MESH)

    def factor_copy(distance):
        to = partner(me_x, distance, n_x)
        return pltpu.make_async_remote_copy(
            src_ref=scales.at[0, to], dst_ref=factors.at[me_x], send_sem=fs_sem.at[distance],
            recv_sem=fr_sem.at[distance], device_id={"gx": to}, device_id_type=MESH)

    def send_x(step, messages, source, piece):
        for message in messages:
            @pl.when(edge(message[2], "gx"))
            def _():
                copy_x(step, message, source, piece).start()

    def send_rows(step, messages):
        for message in messages:
            start, fields, way = message

            @pl.when(edge(way, "gy"))
            def _():
                row = 0 if way < 0 else cy - 1
                for offset, field in enumerate(fields):
                    for x in range(cx):
                        send_y[6 * step + start + offset, pl.ds(x, 1), :] = cur[field, 1 + x, pl.ds(row, 1), :]
                copy_y(step, message).start()

    def finish_sends(step, messages_x, messages_y):
        for message in messages_x:
            @pl.when(edge(message[2], "gx"))
            def _():
                for piece in range(pieces):
                    copy_x(step, message, layer, piece).wait_send()
        for message in messages_y:
            @pl.when(edge(message[2], "gy"))
            def _():
                copy_y(step, message).wait_send()

    def receive_y(step, messages):
        for message in messages:
            start, fields, way = message

            @pl.when(edge(-way, "gy"))
            def _():
                copy_y(step, message).wait_recv()

            @pl.when(jnp.logical_not(edge(-way, "gy")))
            def _():
                for offset in range(len(fields)):
                    halo_y[6 * step + start + offset] = jnp.zeros((cx, cz), jnp.float32)

    def receive_x(step, messages, piece):
        rows = pl.ds(piece * part, part)
        for message in messages:
            start, fields, way = message
            place = cx + 1 if way < 0 else 0

            @pl.when(edge(-way, "gx"))
            def _():
                copy_x(step, message, layer, piece).wait_recv()
                for offset, field in enumerate(fields):
                    cur[field, place, rows, :] = halo_x[6 * step + start + offset, rows, :]

            @pl.when(jnp.logical_not(edge(-way, "gx")))
            def _():
                for field in fields:
                    cur[field, place, rows, :] = jnp.zeros((part, cz), jnp.float32)

    far = max(3 * n_x // 4, 1)

    def send_group(which):
        step, late = which // 2, which % 2
        for distance in range(2, n_x) if n_x > 2 else ():
            if (distance >= far) == (late == 1):
                word_copy(distance, step).start()
        if late == 1:
            word_copy(1, step).start()
        if which == 0:
            for distance in range(1, n_x):
                factor_copy(distance).start()

    def receive_words(step):
        if step == 0:
            own_factor.wait()
            for distance in range(1, n_x):
                factor_copy(distance).wait()
            to_scalar = pltpu.make_async_copy(factors, factor_s, loc_sem.at[0])
            to_scalar.start()
            to_scalar.wait()
        own_words[step].wait()
        for distance in range(1, n_x):
            word_copy(distance, step).wait()

    sub = lax.broadcasted_iota(jnp.int32, (ROWS, cz), 0)
    lane = lax.broadcasted_iota(jnp.int32, (ROWS, cz), 1)
    first_row, last_row = sub == 0, sub == ROWS - 1
    first_lane, last_lane = lane == 0, lane == cz - 1

    def tile(field, x, t):
        return cur[field, x + 1, pl.ds(t * ROWS, ROWS), :]

    def z_before(value):
        return jnp.where(first_lane, 0.0, pltpu.roll(value, 1, 1))

    def z_after(value):
        return jnp.where(last_lane, 0.0, pltpu.roll(value, cz - 1, 1))

    def y_before(value, field, x, t, slot):
        row = halo_y[slot, pl.ds(x, 1), :] if t == 0 else cur[field, x + 1, pl.ds(t * ROWS - 1, 1), :]
        return jnp.where(first_row, jnp.broadcast_to(row, value.shape), pltpu.roll(value, 1, 0))

    def y_after(value, field, x, t, slot):
        row = halo_y[slot, pl.ds(x, 1), :] if t == tiles - 1 else cur[field, x + 1, pl.ds(t * ROWS + ROWS, 1), :]
        return jnp.where(last_row, jnp.broadcast_to(row, value.shape), pltpu.roll(value, ROWS - 1, 0))

    def velocity(step, which, x):
        slot = 6 * step
        for t in which:
            rows = pl.ds(t * ROWS, ROWS)
            scaled = COURANT * coef[0, x, rows, :]
            sxy, sxz, syz = tile(SXY, x, t), tile(SXZ, x, t), tile(SYZ, x, t)
            sxx, syy, szz = tile(SXX, x, t), tile(SYY, x, t), tile(SZZ, x, t)
            moved = (
                tile(VX, x, t) - scaled * (
                    (tile(SXX, x + 1, t) - sxx) + (sxy - y_before(sxy, SXY, x, t, slot + 1)) + (sxz - z_before(sxz))),
                tile(VY, x, t) - scaled * (
                    (sxy - tile(SXY, x - 1, t)) + (y_after(syy, SYY, x, t, slot) - syy) + (syz - z_before(syz))),
                tile(VZ, x, t) - scaled * (
                    (sxz - tile(SXZ, x - 1, t)) + (syz - y_before(syz, SYZ, x, t, slot + 2)) + (z_after(szz) - szz)))
            for field, value in enumerate(moved):
                cur[field, x + 1, rows, :] = value
                if step == STEPS - 1:
                    out[field, x, rows, :] = value

    def stress(step, which, x):
        slot = 6 * step + 3
        for t in which:
            rows = pl.ds(t * ROWS, ROWS)
            vx, vy, vz = tile(VX, x, t), tile(VY, x, t), tile(VZ, x, t)
            exx = vx - tile(VX, x - 1, t)
            eyy = vy - y_before(vy, VY, x, t, slot + 2)
            ezz = vz - z_before(vz)
            exy = (y_after(vx, VX, x, t, slot) - vx) + (tile(VY, x + 1, t) - vy)
            exz = (z_after(vx) - vx) + (tile(VZ, x + 1, t) - vz)
            eyz = (z_after(vy) - vy) + (y_after(vz, VZ, x, t, slot + 1) - vz)
            both = (exx, eyy, ezz, exy, exz, eyz)
            for index, value in enumerate(both):
                strain[6 * step + index, x, rows, :] = value
            pull = (COURANT * coef[1, x, rows, :]) * (exx + eyy + ezz)
            mu = COURANT * coef[2, x, rows, :]
            for index, value in enumerate(both):
                change = pull + (2.0 * mu) * value if index < 3 else mu * value
                moved = tile(SXX + index, x, t) - change
                if step == STEPS - 1:
                    out[SXX + index, x, rows, :] = moved
                else:
                    cur[SXX + index, x + 1, rows, :] = moved

    def over(first, last, body):
        def run(x, carry):
            body(x)
            return carry
        lax.fori_loop(first, last, run, 0)

    def ends(body):
        def run(index, carry):
            body(index * (cx - 1))
            return carry
        lax.fori_loop(0, 2, run, 0)

    width = lanes
    per_x = cy * cz // (4 * segw)

    def source(row, chunk):
        offset = row * cz + chunk * width
        within = offset % (4 * segw)
        return offset // (4 * segw), within % segw, within // segw

    sub_w = lax.broadcasted_iota(jnp.int32, (ROWS, width), 0)

    def gradient(step, x):
        made = {}
        for t in range(tiles):
            for chunk in range(cz // width):
                rows = pl.ds(t * ROWS, ROWS)
                columns = pl.ds(chunk * width, width)
                plan = [source(t * ROWS + r, chunk) for r in range(ROWS)]
                shift = jnp.full((ROWS, width), 8 * plan[0][2], jnp.int32)
                for r in range(1, ROWS):
                    if plan[r][2] != plan[r - 1][2]:
                        shift = jnp.where(sub_w >= r, 8 * plan[r][2], shift)
                key = tuple(p[:2] for p in plan)
                distinct = list(dict.fromkeys(key))
                masks = []
                for item in distinct[1:]:
                    mask = None
                    for r in range(ROWS):
                        if key[r] == item:
                            mask = (sub_w == r) if mask is None else mask | (sub_w == r)
                    masks.append(mask)
                holders = {b: inv[x * per_x + b] for b in dict.fromkeys(k[0] for k in key)}
                blocks = [k[0] for k in key]

                def stored(c):
                    if (key, c) not in made:
                        word = None
                        for position, (block, start) in enumerate(distinct):
                            piece = jnp.broadcast_to(
                                words[step][holders[block], c - per_step * step, pl.ds(start // lanes, 1), :], (ROWS, width))
                            word = piece if word is None else jnp.where(masks[position - 1], piece, word)
                        made[key, c] = word ^ jnp.int32(-2147483648)
                    byte = (lax.shift_right_logical(made[key, c], shift) & 255) - 128
                    factor = None
                    for r in range(ROWS):
                        if r == 0:
                            factor = factor_s[holders[blocks[0]], 0, c]
                        elif blocks[r] != blocks[r - 1]:
                            factor = jnp.where(sub_w >= r, factor_s[holders[blocks[r]], 0, c], factor)
                    return byte.astype(jnp.float32) * factor

                e = [strain[6 * step + index, x, rows, columns] for index in range(6)]
                f = [stored(6 * step + index) for index in range(6)]
                grad_lambda = (e[0] + e[1] + e[2]) * (f[0] + f[1] + f[2])
                grad_mu = 2.0 * (e[0] * f[0] + e[1] * f[1] + e[2] * f[2])
                grad_mu = grad_mu + e[3] * f[3] + e[4] * f[4] + e[5] * f[5]
                if step > 0:
                    grad_lambda = grads[0, x, rows, columns] + grad_lambda
                    grad_mu = grads[1, x, rows, columns] + grad_mu
                grads[0, x, rows, columns] = grad_lambda
                grads[1, x, rows, columns] = grad_mu

    def inside(piece):
        return range(piece * part // ROWS, (piece + 1) * part // ROWS)

    outer = (0, tiles - 1) if tiles > 1 else (0,)
    inner = range(1, tiles - 1)

    for step in range(STEPS):
        if step == 0:
            for piece in range(pieces):
                send_x(0, STRESS_X, first_layer, piece)
            for copy in loads:
                copy.wait()
            send_rows(0, STRESS_Y)
            send_group(0)
            def invert(block, carry):
                total = jnp.int32(0)
                for holder in range(n_x):
                    total = jnp.where(perm[0, holder] == block, holder, total)
                inv[block] = total
                return carry
            lax.fori_loop(0, n_x, invert, 0)
        if step > 0:
            finish_sends(step - 1, SPEED_X, SPEED_Y)
        receive_y(step, STRESS_Y)
        for piece in range(pieces):
            receive_x(step, STRESS_X, piece)
            ends(functools.partial(velocity, step, inside(piece)))
            send_x(step, SPEED_X, layer, piece)
        over(1, cx - 1, functools.partial(velocity, step, outer))
        send_rows(step, SPEED_Y)
        over(1, cx - 1, functools.partial(velocity, step, inner))
        send_group(1 + 2 * step)
        if step > 0:
            receive_words(step - 1)
            over(0, cx, functools.partial(gradient, step - 1))
        finish_sends(step, STRESS_X, STRESS_Y)
        receive_y(step, SPEED_Y)
        for piece in range(pieces):
            receive_x(step, SPEED_X, piece)
            ends(functools.partial(stress, step, inside(piece)))
            if step < STEPS - 1:
                send_x(step + 1, STRESS_X, layer, piece)
        over(1, cx - 1, functools.partial(stress, step, outer))
        if step < STEPS - 1:
            send_rows(step + 1, STRESS_Y)
        over(1, cx - 1, functools.partial(stress, step, inner))
        if step < STEPS - 1:
            send_group(2 + 2 * step)
    finish_sends(STEPS - 1, SPEED_X, SPEED_Y)
    receive_words(STEPS - 1)
    over(0, cx, functools.partial(gradient, STEPS - 1))


def on_device(n_x, n_y, adjoint, buoyancy, lame_lambda, shear_mu, packed, scales, perm):
    fields, cx, cy, cz = adjoint.shape
    comp, segw = packed.shape[3:]
    lanes = min(128, segw)
    packed = packed.reshape(n_x, comp, segw // lanes, lanes)
    halos = 6 * STEPS
    pieces = PIECES if cy % (PIECES * ROWS) == 0 else 1
    dma = pltpu.SemaphoreType.DMA
    return pl.pallas_call(
        functools.partial(kernel, n_x, n_y),
        out_shape=(pltpu.VMEM(adjoint.shape, jnp.float32), pltpu.VMEM((2, cx, cy, cz), jnp.float32)),
        in_specs=[pl.BlockSpec(memory_space=pltpu.HBM)] * 6 + [pl.BlockSpec(memory_space=pltpu.SMEM)],
        out_specs=(pl.BlockSpec(memory_space=pltpu.VMEM),) * 2,
        scratch_shapes=[
            pltpu.VMEM((fields, cx + 2, cy, cz), jnp.float32),
            pltpu.VMEM((3, cx, cy, cz), jnp.float32),
            pltpu.VMEM((comp, cx, cy, cz), jnp.float32),
            pltpu.VMEM((halos, cy, cz), jnp.float32),
            pltpu.VMEM((halos, cx, cz), jnp.float32),
            pltpu.VMEM((halos, cx, cz), jnp.float32),
            pltpu.VMEM((n_x, 1, comp), jnp.float32),
            pltpu.SMEM((n_x, 1, comp), jnp.float32),
            pltpu.SMEM((n_x,), jnp.int32),
            dma((12,)), dma((halos, pieces)), dma((halos, pieces)), dma((halos,)), dma((halos,)),
            dma((n_x, STEPS)), dma((n_x, STEPS)), dma((n_x,)), dma((n_x,)), dma((2 + STEPS,)),
        ] + [pltpu.VMEM((n_x, comp // STEPS, segw // lanes, lanes), jnp.int32)] * STEPS,
        compiler_params=pltpu.CompilerParams(collective_id=0, has_side_effects=True,
                                             vmem_limit_bytes=64000000),
    )(adjoint, buoyancy, lame_lambda, shear_mu, packed, scales, perm)


def solution(mesh):
    return jax.shard_map(
        functools.partial(on_device, mesh.shape["gx"], mesh.shape["gy"]),
        mesh=mesh,
        in_specs=(
            P(None, "gx", "gy", None),
            P("gx", "gy", None),
            P("gx", "gy", None),
            P("gx", "gy", None),
            P("gx", None, "gy", None, None),
            P("gx", None, "gy", None),
            P("gx", None),
        ),
        out_specs=(P(None, "gx", "gy", None), P(None, "gx", "gy", None)),
        check_vma=False,
    )
```

profile of v0, /device:TPU:2, one launch (start us, length us, event | category | flops | bytes accessed | tf_op | source)
XLA Modules:
  0.0 57.7 jit_solution(280788213547999704)
XLA Ops:
  0.6 1.4 %copy.9.scales = f32[1,64,1,12]{3,2,1,0:T(1,128)} copy(f32[1,64,1,12]{1,2,3,0:T(1,128)} %param.12) | data formatting | bytes 6144 | tf_op args[5]
  2.0 53.5 %shard_map.86 = (f32[9,4,32,512]{3,2,1,0:T(8,128)S(1)}, f32[2,4,32,512]{3,2,1,0:T(8,128)S(1)}) custom-call(f32[9,4,32,512]{3,2,1,0:T(8,128)} %adj.1, f32[4,32,512]{2,1,0:T(8,128)} %buoy.1, f32[4,32,512]{2,1,0:T(8,128)} %lam.1, f32[4,32,512]{2,1,0:T(8,128)} %shear.1, s32[64,12,2,128]{3,2,1,0:T(2,128)} %bitcast.1, f32[1,64,1,12]{3,2,1,0:T(1,128)} %copy.9.scales, ...), custom_call_target="tpu_custom_call" | custom-call | tf_op jit(solution)/shard_map/pallas_call | solution.py:396
  55.5 1.4 %copy.12 = f32[9,4,32,512]{3,2,1,0:T(8,128)} copy(f32[9,4,32,512]{3,2,1,0:T(8,128)S(1)} %get-tuple-element.2) | data formatting | bytes 4718592
  57.0 0.8 %copy.13 = f32[2,4,32,512]{3,2,1,0:T(8,128)} copy(f32[2,4,32,512]{3,2,1,0:T(8,128)S(1)} %get-tuple-element.3) | data formatting | bytes 1048576
where the time goes:
time: 57.9 us; the launch traced here: 57.7 us
  Pallas kernels  53.5 us (92%)
  local copies, waits for them, and re-layouts  3.59 us (6%)
  between operations  0.64 us (1%)
    pallas_call x1, Pallas kernels, on_device(): pl.pallas_call(functools.partial(kernel, n_x, n_y), out_shape=(pltpu.VMEM...  53.5 us
    unnamed x3, local copies, waits for them, and re-layouts  3.59 us

commit v1 on v0

v1 whole, which is shorter than its diff:
```python
import functools

import jax
import jax.numpy as jnp
from jax import lax
from jax.experimental import pallas as pl
from jax.experimental.pallas import tpu as pltpu
from jax.sharding import PartitionSpec as P

MESH = pl.DeviceIdType.MESH
STEPS = 2
COURANT = 0.15
ROWS = 8
ZBIT = 8

VX, VY, VZ, SXX, SYY, SZZ, SXY, SXZ, SYZ = range(9)

DOWN_S, DOWN_V, DOWN_B, DOWN_C, UP_S, UP_V, UP_B, UP_C = range(8)
STRESS_Y = ((0, (SYY,), -1), (1, (SXY, SYZ), 1))
SPEED_Y = ((3, (VX, VZ), -1), (5, (VY,), 1))


def partner(me, distance, count):
    if count & (count - 1):
        return lax.rem(me + distance, count)
    result, bit = me, 1
    while bit < count:
        if distance & bit:
            result = result + bit - 2 * bit * ((me // bit) % 2)
        bit *= 2
    return result


def kernel(n_x, n_y, adj, buoy, lam, shear, packed, scales, perm, out, grads,
           cur, coef, strain, halo_x, halo_b, part, corner, corner_send, halo_y, send_y, late_y, late_send,
           table, scale_v, factor_send, factors, factor_s, perm_v, inv_v, inv,
           in_sem, xs_sem, xr_sem, ys_sem, yr_sem, ws_sem, wr_sem, fs_sem, fr_sem, loc_sem, *words):
    cx, cy, cz = buoy.shape
    comp = packed.shape[1]
    per_step = comp // STEPS
    lanes = packed.shape[3]
    segw = packed.shape[2] * lanes
    tiles = cy // ROWS
    last = cx - 1
    me_x, me_y = lax.axis_index("gx"), lax.axis_index("gy")

    barrier = pltpu.get_barrier_semaphore()
    for distance in range(1, n_x):
        pl.semaphore_signal(barrier, inc=1, device_id={"gx": partner(me_x, distance, n_x)}, device_id_type=MESH)

    def edge(way, axis):
        me, count = (me_x, n_x) if axis == "gx" else (me_y, n_y)
        return (me > 0) if way < 0 else (me < count - 1)

    for way in (-1, 1):
        @pl.when(edge(way, "gy"))
        def _():
            pl.semaphore_signal(barrier, inc=1, device_id={"gy": me_y + way}, device_id_type=MESH)

    loads = {}
    for index in (SXX, SXY, SXZ, SYY, SYZ, SZZ, VX, VY, VZ):
        loads[index] = pltpu.make_async_copy(adj.at[index], cur.at[index, pl.ds(1, cx)], in_sem.at[index])
    for index, ref in enumerate((buoy, lam, shear)):
        loads[9 + index] = pltpu.make_async_copy(ref, coef.at[index], in_sem.at[9 + index])
    load_perm = pltpu.make_async_copy(perm, perm_v, loc_sem.at[0])
    load_scales = pltpu.make_async_copy(scales, scale_v, loc_sem.at[1])
    own_words = [pltpu.make_async_copy(packed.at[me_x, pl.ds(step * per_step, per_step)], words[step].at[me_x],
                                       loc_sem.at[2 + step]) for step in range(STEPS)]
    for index in (9, SXY, SXZ, SYZ, SXX, SYY, SZZ, VX, VY, VZ, 10, 11):
        loads[index].start()
    load_perm.start()
    load_scales.start()
    for copy in own_words:
        copy.start()

    def x_copy(step, kind):
        way = 1 if kind < UP_S else -1
        if kind == DOWN_S:
            fields = pl.ds(SXY, 2)
            src = adj.at[fields, last] if step == 0 else cur.at[fields, cx]
            dst = halo_x.at[step, pl.ds(0, 2)]
        elif kind == DOWN_V:
            src, dst = part.at[step, pl.ds(0, 1)], halo_x.at[step, pl.ds(2, 1)]
        elif kind == DOWN_B:
            src, dst = buoy.at[last], halo_b.at[0]
        elif kind == DOWN_C:
            src, dst = corner_send.at[step, pl.ds(0, 1)], corner.at[step, pl.ds(0, 1)]
        elif kind == UP_S:
            src, dst = (adj.at[SXX, 0] if step == 0 else cur.at[SXX, 1]), halo_x.at[step, 3]
        elif kind == UP_V:
            src, dst = part.at[step, pl.ds(1, 2)], halo_x.at[step, pl.ds(4, 2)]
        elif kind == UP_B:
            src, dst = buoy.at[0], halo_b.at[1]
        else:
            src, dst = corner_send.at[step, pl.ds(1, 2)], corner.at[step, pl.ds(1, 2)]
        return way, pltpu.make_async_remote_copy(
            src_ref=src, dst_ref=dst, send_sem=xs_sem.at[step, kind], recv_sem=xr_sem.at[step, kind],
            device_id={"gx": me_x + way}, device_id_type=MESH)

    def x_start(step, *kinds):
        for kinds_way, way in ((kinds[:], 1), (kinds[:], -1)):
            mine = [k for k in kinds_way if (k < UP_S) == (way == 1)]
            if mine:
                @pl.when(edge(way, "gx"))
                def _():
                    for kind in mine:
                        x_copy(step, kind)[1].start()

    def x_wait(step, what, *kinds):
        for way in (1, -1):
            mine = [k for k in kinds if (k < UP_S) == (way == 1)]
            if mine:
                @pl.when(edge(-way if what == "recv" else way, "gx"))
                def _():
                    for kind in mine:
                        copy = x_copy(step, kind)[1]
                        if what == "recv":
                            copy.wait_recv()
                        else:
                            copy.wait_send()

    def y_copy(step, message):
        start, fields, way = message
        slot = 6 * step + start
        return pltpu.make_async_remote_copy(
            src_ref=send_y.at[pl.ds(slot, len(fields))], dst_ref=halo_y.at[pl.ds(slot, len(fields))],
            send_sem=ys_sem.at[slot], recv_sem=yr_sem.at[slot],
            device_id={"gy": me_y + way}, device_id_type=MESH)

    def late(step, which):
        way = -1 if which == 0 else 1
        first, count = (3 * step, 2) if which == 0 else (3 * step + 2, 1)
        sem = 6 * STEPS + 2 * step + which
        return way, pltpu.make_async_remote_copy(
            src_ref=late_send.at[pl.ds(first, count)], dst_ref=late_y.at[pl.ds(first, count)],
            send_sem=ys_sem.at[sem], recv_sem=yr_sem.at[sem],
            device_id={"gy": me_y + way}, device_id_type=MESH)

    def send_rows(step, messages):
        for message in messages:
            start, fields, way = message

            @pl.when(edge(way, "gy"))
            def _():
                row = 0 if way < 0 else cy - 1
                for offset, field in enumerate(fields):
                    for x in range(cx):
                        send_y[6 * step + start + offset, pl.ds(x, 1), :] = cur[field, 1 + x, pl.ds(row, 1), :]
                y_copy(step, message).start()

    def receive_y(step, messages):
        for message in messages:
            @pl.when(edge(-message[2], "gy"))
            def _():
                y_copy(step, message).wait_recv()

    def send_late(step):
        @pl.when(edge(-1, "gy"))
        def _():
            late_send[3 * step] = cur[VX, cx, pl.ds(0, 1), :]
            late_send[3 * step + 1] = cur[VZ, 1, pl.ds(0, 1), :]
            late(step, 0)[1].start()

        @pl.when(edge(1, "gy"))
        def _():
            late_send[3 * step + 2] = cur[VY, 1, pl.ds(cy - 1, 1), :]
            late(step, 1)[1].start()

    def receive_late(step):
        @pl.when(edge(1, "gy"))
        def _():
            late(step, 0)[1].wait_recv()
            halo_y[6 * step + 3, pl.ds(last, 1), :] = late_y[3 * step]
            halo_y[6 * step + 4, pl.ds(0, 1), :] = late_y[3 * step + 1]

        @pl.when(edge(-1, "gy"))
        def _():
            late(step, 1)[1].wait_recv()
            halo_y[6 * step + 5, pl.ds(0, 1), :] = late_y[3 * step + 2]

    def forward_corners(step):
        slot = 6 * step
        corner_send[step, 0] = halo_y[slot + 1, pl.ds(last, 1), :]
        corner_send[step, 1] = halo_y[slot, pl.ds(0, 1), :]
        corner_send[step, 2] = halo_y[slot + 2, pl.ds(0, 1), :]
        x_start(step, DOWN_C, UP_C)

    def word_copy(distance, step):
        to = partner(me_x, distance, n_x)
        stored = pl.ds(step * per_step, per_step)
        return pltpu.make_async_remote_copy(
            src_ref=packed.at[to, stored], dst_ref=words[step].at[me_x], send_sem=ws_sem.at[distance, step],
            recv_sem=wr_sem.at[distance, step], device_id={"gx": to}, device_id_type=MESH)

    def factor_copy(distance):
        to = partner(me_x, distance, n_x)
        return pltpu.make_async_remote_copy(
            src_ref=factor_send.at[to], dst_ref=factors.at[me_x], send_sem=fs_sem.at[distance],
            recv_sem=fr_sem.at[distance], device_id={"gx": to}, device_id_type=MESH)

    far = [d for d in range(1, n_x) if d & ZBIT]
    near = [d for d in range(1, n_x) if not d & ZBIT]

    def send_words(step, distances):
        for distance in distances:
            word_copy(distance, step).start()

    def receive_words(step):
        own_words[step].wait()
        for distance in near + far:
            word_copy(distance, step).wait()

    sub = lax.broadcasted_iota(jnp.int32, (ROWS, cz), 0)
    lane = lax.broadcasted_iota(jnp.int32, (ROWS, cz), 1)
    first_row, last_row = sub == 0, sub == ROWS - 1
    first_lane, last_lane = lane == 0, lane == cz - 1

    def tile(field, x, t):
        return cur[field, x + 1, pl.ds(t * ROWS, ROWS), :]

    def z_before(value):
        return jnp.where(first_lane, 0.0, pltpu.roll(value, 1, 1))

    def z_after(value):
        return jnp.where(last_lane, 0.0, pltpu.roll(value, cz - 1, 1))

    def y_before(value, field, x, t, slot):
        if t == 0:
            row = None if slot is None else halo_y[slot, pl.ds(x, 1), :]
        else:
            row = cur[field, x + 1, pl.ds(t * ROWS - 1, 1), :]
        row = 0.0 if row is None else jnp.broadcast_to(row, value.shape)
        return jnp.where(first_row, row, pltpu.roll(value, 1, 0))

    def y_after(value, field, x, t, slot):
        if t == tiles - 1:
            row = None if slot is None else halo_y[slot, pl.ds(x, 1), :]
        else:
            row = cur[field, x + 1, pl.ds(t * ROWS + ROWS, 1), :]
        row = 0.0 if row is None else jnp.broadcast_to(row, value.shape)
        return jnp.where(last_row, row, pltpu.roll(value, ROWS - 1, 0))

    def keep(step, field, x, rows, value):
        cur[field, x + 1, rows, :] = value
        if step == STEPS - 1:
            out[field, x, rows, :] = value

    def partials(step):
        for t in range(tiles):
            rows = pl.ds(t * ROWS, ROWS)
            sxx, sxy, sxz = tile(SXX, last, t), tile(SXY, last, t), tile(SXZ, last, t)
            part[step, 0, rows, :] = tile(VX, last, t) - (COURANT * coef[0, last, rows, :]) * (
                (sxy - y_before(sxy, SXY, last, t, None)) + (sxz - z_before(sxz)) - sxx)
        for t in range(tiles):
            rows = pl.ds(t * ROWS, ROWS)
            scaled = COURANT * coef[0, 0, rows, :]
            sxy, sxz, syz = tile(SXY, 0, t), tile(SXZ, 0, t), tile(SYZ, 0, t)
            syy, szz = tile(SYY, 0, t), tile(SZZ, 0, t)
            part[step, 1, rows, :] = tile(VY, 0, t) - scaled * (
                sxy + (y_after(syy, SYY, 0, t, None) - syy) + (syz - z_before(syz)))
            part[step, 2, rows, :] = tile(VZ, 0, t) - scaled * (
                sxz + (syz - y_before(syz, SYZ, 0, t, None)) + (z_after(szz) - szz))

    def velocity(step, which, x, want=(VX, VY, VZ)):
        slot = 6 * step
        for t in which:
            rows = pl.ds(t * ROWS, ROWS)
            scaled = COURANT * coef[0, x, rows, :]
            sxy, sxz = tile(SXY, x, t), tile(SXZ, x, t)
            if VX in want:
                keep(step, VX, x, rows, tile(VX, x, t) - scaled * (
                    (tile(SXX, x + 1, t) - tile(SXX, x, t)) + (sxy - y_before(sxy, SXY, x, t, slot + 1))
                    + (sxz - z_before(sxz))))
            if VY in want:
                syy, syz, szz = tile(SYY, x, t), tile(SYZ, x, t), tile(SZZ, x, t)
                keep(step, VY, x, rows, tile(VY, x, t) - scaled * (
                    (sxy - tile(SXY, x - 1, t)) + (y_after(syy, SYY, x, t, slot) - syy) + (syz - z_before(syz))))
                keep(step, VZ, x, rows, tile(VZ, x, t) - scaled * (
                    (sxz - tile(SXZ, x - 1, t)) + (syz - y_before(syz, SYZ, x, t, slot + 2)) + (z_after(szz) - szz)))

    def complete(step):
        slot = 6 * step
        for t in range(tiles):
            rows = pl.ds(t * ROWS, ROWS)

            def edge_row(value, row, at):
                return value + jnp.where(at, jnp.broadcast_to(row, (ROWS, cz)), 0.0)

            scaled = COURANT * coef[0, last, rows, :]
            more = halo_x[step, 3, rows, :]
            if t == 0:
                more = edge_row(more, -halo_y[slot + 1, pl.ds(last, 1), :], first_row)
            keep(step, VX, last, rows, part[step, 0, rows, :] - scaled * more)

            scaled = COURANT * coef[0, 0, rows, :]
            more = halo_x[step, 0, rows, :]
            if t == tiles - 1:
                more = edge_row(more, -halo_y[slot, pl.ds(0, 1), :], last_row)
            keep(step, VY, 0, rows, part[step, 1, rows, :] + scaled * more)
            more = halo_x[step, 1, rows, :]
            if t == 0:
                more = edge_row(more, halo_y[slot + 2, pl.ds(0, 1), :], first_row)
            keep(step, VZ, 0, rows, part[step, 2, rows, :] + scaled * more)

            more = tile(SXX, 0, t)
            if t == 0:
                more = edge_row(more, -corner[step, 0], first_row)
            cur[VX, 0, rows, :] = halo_x[step, 2, rows, :] - (COURANT * halo_b[0, rows, :]) * more

            scaled = COURANT * halo_b[1, rows, :]
            more = tile(SXY, last, t)
            if t == tiles - 1:
                more = edge_row(more, -corner[step, 1], last_row)
            cur[VY, cx + 1, rows, :] = halo_x[step, 4, rows, :] + scaled * more
            more = tile(SXZ, last, t)
            if t == 0:
                more = edge_row(more, corner[step, 2], first_row)
            cur[VZ, cx + 1, rows, :] = halo_x[step, 5, rows, :] + scaled * more

    def stress(step, which, x):
        slot = 6 * step + 3
        for t in which:
            rows = pl.ds(t * ROWS, ROWS)
            vx, vy, vz = tile(VX, x, t), tile(VY, x, t), tile(VZ, x, t)
            exx = vx - tile(VX, x - 1, t)
            eyy = vy - y_before(vy, VY, x, t, slot + 2)
            ezz = vz - z_before(vz)
            exy = (y_after(vx, VX, x, t, slot) - vx) + (tile(VY, x + 1, t) - vy)
            exz = (z_after(vx) - vx) + (tile(VZ, x + 1, t) - vz)
            eyz = (z_after(vy) - vy) + (y_after(vz, VZ, x, t, slot + 1) - vz)
            both = (exx, eyy, ezz, exy, exz, eyz)
            for index, value in enumerate(both):
                strain[6 * step + index, x, rows, :] = value
            pull = (COURANT * coef[1, x, rows, :]) * (exx + eyy + ezz)
            mu = COURANT * coef[2, x, rows, :]
            for index, value in enumerate(both):
                change = pull + (2.0 * mu) * value if index < 3 else mu * value
                moved = tile(SXX + index, x, t) - change
                if step == STEPS - 1:
                    out[SXX + index, x, rows, :] = moved
                else:
                    cur[SXX + index, x + 1, rows, :] = moved

    def over(first, stop, body):
        def run(x, carry):
            body(x)
            return carry
        lax.fori_loop(first, stop, run, 0)

    def ends(body):
        def run(index, carry):
            body(index * (cx - 1))
            return carry
        lax.fori_loop(0, 2, run, 0)

    width = lanes
    per_x = cy * cz // (4 * segw)

    def source(row, chunk):
        offset = row * cz + chunk * width
        within = offset % (4 * segw)
        return offset // (4 * segw), within % segw, within // segw

    sub_w = lax.broadcasted_iota(jnp.int32, (ROWS, width), 0)

    def gradient(step, x):
        made = {}
        for t in range(tiles):
            for chunk in range(cz // width):
                rows = pl.ds(t * ROWS, ROWS)
                columns = pl.ds(chunk * width, width)
                plan = [source(t * ROWS + r, chunk) for r in range(ROWS)]
                shift = jnp.full((ROWS, width), 8 * plan[0][2], jnp.int32)
                for r in range(1, ROWS):
                    if plan[r][2] != plan[r - 1][2]:
                        shift = jnp.where(sub_w >= r, 8 * plan[r][2], shift)
                key = tuple(p[:2] for p in plan)
                distinct = list(dict.fromkeys(key))
                masks = []
                for item in distinct[1:]:
                    mask = None
                    for r in range(ROWS):
                        if key[r] == item:
                            mask = (sub_w == r) if mask is None else mask | (sub_w == r)
                    masks.append(mask)
                holders = {b: inv[0, x * per_x + b] for b in dict.fromkeys(k[0] for k in key)}
                blocks = [k[0] for k in key]

                def stored(c):
                    if (key, c) not in made:
                        word = None
                        for position, (block, start) in enumerate(distinct):
                            piece = jnp.broadcast_to(
                                words[step][holders[block], c - per_step * step, pl.ds(start // lanes, 1), :], (ROWS, width))
                            word = piece if word is None else jnp.where(masks[position - 1], piece, word)
                        made[key, c] = word ^ jnp.int32(-2147483648)
                    byte = (lax.shift_right_logical(made[key, c], shift) & 255) - 128
                    factor = None
                    for r in range(ROWS):
                        if r == 0:
                            factor = factor_s[holders[blocks[0]], 0, c]
                        elif blocks[r] != blocks[r - 1]:
                            factor = jnp.where(sub_w >= r, factor_s[holders[blocks[r]], 0, c], factor)
                    return byte.astype(jnp.float32) * factor

                e = [strain[6 * step + index, x, rows, columns] for index in range(6)]
                f = [stored(6 * step + index) for index in range(6)]
                grad_lambda = (e[0] + e[1] + e[2]) * (f[0] + f[1] + f[2])
                grad_mu = 2.0 * (e[0] * f[0] + e[1] * f[1] + e[2] * f[2])
                grad_mu = grad_mu + e[3] * f[3] + e[4] * f[4] + e[5] * f[5]
                if step > 0:
                    grad_lambda = grads[0, x, rows, columns] + grad_lambda
                    grad_mu = grads[1, x, rows, columns] + grad_mu
                grads[0, x, rows, columns] = grad_lambda
                grads[1, x, rows, columns] = grad_mu

    for way in (-1, 1):
        @pl.when(jnp.logical_not(edge(way, "gx")))
        def _():
            zero = jnp.zeros((ROWS, cz), jnp.float32)
            for t in range(tiles):
                rows = pl.ds(t * ROWS, ROWS)
                halo_b[0 if way < 0 else 1, rows, :] = zero
                for step in range(STEPS):
                    for slot in (0, 1, 2) if way < 0 else (3, 4, 5):
                        halo_x[step, slot, rows, :] = zero
            for step in range(STEPS):
                for slot in (0,) if way < 0 else (1, 2):
                    corner[step, slot] = jnp.zeros((1, cz), jnp.float32)

        @pl.when(jnp.logical_not(edge(way, "gy")))
        def _():
            for step in range(STEPS):
                for start, fields, sent in STRESS_Y + SPEED_Y:
                    if sent == -way:
                        for offset in range(len(fields)):
                            halo_y[6 * step + start + offset] = jnp.zeros((cx, cz), jnp.float32)

    outer = (0, tiles - 1) if tiles > 1 else (0,)
    inner = range(1, tiles - 1)
    every = range(tiles)
    waited = set()

    def need(*which):
        for index in which:
            if index not in waited:
                loads[index].wait()
                waited.add(index)

    need(*range(12))
    partials(0)

    pl.semaphore_wait(barrier, n_x - 1 + jnp.minimum(me_y, 1) + jnp.minimum(n_y - 1 - me_y, 1))

    x_start(0, DOWN_S, UP_S, DOWN_V, UP_V, DOWN_B, UP_B)
    send_rows(0, STRESS_Y)
    send_words(0, near)

    load_scales.wait()
    load_perm.wait()
    square = 128
    sub_q = lax.broadcasted_iota(jnp.int32, (square, square), 0)
    lane_q = lax.broadcasted_iota(jnp.int32, (square, square), 1)
    table[...] = jnp.zeros((16, square), jnp.float32)
    for c in range(comp):
        table[pl.ds(c, 1), pl.ds(0, n_x)] = scale_v[c]
    by_owner = jnp.transpose(jnp.concatenate([table[...], jnp.zeros((square - 16, square), jnp.float32)], axis=0))
    for owner in range(n_x):
        factor_send[owner] = by_owner[owner:owner + 1, :comp]
    inv_v[...] = jnp.full((1, square), -1, jnp.int32)
    inv_v[pl.ds(0, 1), pl.ds(0, n_x)] = perm_v[...]
    by_holder = jnp.transpose(jnp.broadcast_to(inv_v[...], (square, square)))
    inv_v[...] = jnp.max(jnp.where(by_holder == lane_q, sub_q, 0), axis=0, keepdims=True)
    inverse = pltpu.make_async_copy(inv_v, inv, loc_sem.at[0])
    inverse.start()
    own_factor = pltpu.make_async_copy(factor_send.at[me_x], factors.at[me_x], loc_sem.at[1])
    own_factor.start()

    half = len(far) // 2
    for step in range(STEPS):
        if step > 0:
            partials(step)
            x_start(step, DOWN_S, UP_S, DOWN_V, UP_V)
            send_rows(step, STRESS_Y)
            send_words(step, far)
            send_words(step, near)
        receive_y(step, STRESS_Y)
        forward_corners(step)
        velocity(step, every, 0, (VX,))
        velocity(step, every, last, (VY, VZ))
        over(1, last, functools.partial(velocity, step, every))
        send_rows(step, SPEED_Y)
        if step == 0:
            send_words(0, far[:half])
            for distance in near + far:
                factor_copy(distance).start()
        receive_y(step, SPEED_Y)
        over(1, last, functools.partial(stress, step, every))
        if step > 0:
            own_factor.wait()
            for distance in near + far:
                factor_copy(distance).wait()
            to_scalar = pltpu.make_async_copy(factors, factor_s, loc_sem.at[1])
            to_scalar.start()
            to_scalar.wait()
            inverse.wait()
            receive_words(step - 1)
            over(0, cx, functools.partial(gradient, step - 1))
        x_wait(step, "recv", DOWN_S, DOWN_V, DOWN_C, UP_S, UP_V, UP_C)
        if step == 0:
            x_wait(0, "recv", DOWN_B, UP_B)
        complete(step)
        send_late(step)
        if step == 0:
            send_words(0, far[half:])
        ends(functools.partial(stress, step, inner))
        receive_late(step)
        ends(functools.partial(stress, step, outer))
    receive_words(STEPS - 1)
    over(0, cx, functools.partial(gradient, STEPS - 1))

    for step in range(STEPS):
        x_wait(step, "send", DOWN_S, DOWN_V, DOWN_C, UP_S, UP_V, UP_C)
        for message in STRESS_Y + SPEED_Y:
            @pl.when(edge(message[2], "gy"))
            def _():
                y_copy(step, message).wait_send()
        for which in (0, 1):
            way, copy = late(step, which)

            @pl.when(edge(way, "gy"))
            def _():
                copy.wait_send()
    x_wait(0, "send", DOWN_B, UP_B)


def on_device(n_x, n_y, adjoint, buoyancy, lame_lambda, shear_mu, packed, scales, perm):
    fields, cx, cy, cz = adjoint.shape
    comp, segw = packed.shape[3:]
    lanes = min(128, segw)
    packed = packed.reshape(n_x, comp, segw // lanes, lanes)
    scales = jnp.transpose(scales, (0, 3, 2, 1)).reshape(comp, 1, n_x)
    halos = 6 * STEPS
    dma = pltpu.SemaphoreType.DMA
    f32, i32 = jnp.float32, jnp.int32
    return pl.pallas_call(
        functools.partial(kernel, n_x, n_y),
        out_shape=(pltpu.VMEM(adjoint.shape, f32), pltpu.VMEM((2, cx, cy, cz), f32)),
        in_specs=[pl.BlockSpec(memory_space=pltpu.HBM)] * 7,
        out_specs=(pl.BlockSpec(memory_space=pltpu.VMEM),) * 2,
        scratch_shapes=[
            pltpu.VMEM((fields, cx + 2, cy, cz), f32),
            pltpu.VMEM((3, cx, cy, cz), f32),
            pltpu.VMEM((comp, cx, cy, cz), f32),
            pltpu.VMEM((STEPS, 6, cy, cz), f32),
            pltpu.VMEM((2, cy, cz), f32),
            pltpu.VMEM((STEPS, 3, cy, cz), f32),
            pltpu.VMEM((STEPS, 3, 1, cz), f32),
            pltpu.VMEM((STEPS, 3, 1, cz), f32),
            pltpu.VMEM((halos, cx, cz), f32),
            pltpu.VMEM((halos, cx, cz), f32),
            pltpu.VMEM((3 * STEPS, 1, cz), f32),
            pltpu.VMEM((3 * STEPS, 1, cz), f32),
            pltpu.VMEM((16, 128), f32),
            pltpu.VMEM((comp, 1, n_x), f32),
            pltpu.VMEM((n_x, 1, comp), f32),
            pltpu.VMEM((n_x, 1, comp), f32),
            pltpu.SMEM((n_x, 1, comp), f32),
            pltpu.VMEM((1, n_x), i32),
            pltpu.VMEM((1, 128), i32),
            pltpu.SMEM((1, 128), i32),
            dma((12,)), dma((STEPS, 8)), dma((STEPS, 8)), dma((halos + 2 * STEPS,)), dma((halos + 2 * STEPS,)),
            dma((n_x, STEPS)), dma((n_x, STEPS)), dma((n_x,)), dma((n_x,)), dma((2 + STEPS,)),
        ] + [pltpu.VMEM((n_x, comp // STEPS, segw // lanes, lanes), i32)] * STEPS,
        compiler_params=pltpu.CompilerParams(collective_id=0, has_side_effects=True,
                                             vmem_limit_bytes=64000000),
    )(adjoint, buoyancy, lame_lambda, shear_mu, packed, scales, perm)


def solution(mesh):
    return jax.shard_map(
        functools.partial(on_device, mesh.shape["gx"], mesh.shape["gy"]),
        mesh=mesh,
        in_specs=(
            P(None, "gx", "gy", None),
            P("gx", "gy", None),
            P("gx", "gy", None),
            P("gx", "gy", None),
            P("gx", None, "gy", None, None),
            P("gx", None, "gy", None),
            P("gx", None),
        ),
        out_specs=(P(None, "gx", "gy", None), P(None, "gx", "gy", None)),
        check_vma=False,
    )
```

time: 57.9 us -> 60.9 us (1.052)
  Pallas kernels: 53.5 us -> 58 us
  local copies, waits for them, and re-layouts: 3.59 us -> 2.2 us
    pallas_call x1, Pallas kernels: 53.5 us -> 58 us  [on_device(): pl.pallas_call(functools.partial(kernel, n_x, n_y), out_shape=(pltpu.VMEM...]
    unnamed x3 -> x2, local copies, waits for them, and re-layouts: 3.59 us -> 2.2 us
where the time goes in v1:
time: 60.9 us; the launch traced here: 60.8 us
  Pallas kernels  58 us (95%)
  local copies, waits for them, and re-layouts  2.2 us (4%)
  between operations  0.64 us (1%)
    pallas_call x1, Pallas kernels, on_device(): pl.pallas_call(functools.partial(kernel, n_x, n_y), out_shape=(pltpu.VMEM...  58 us
    unnamed x2, local copies, waits for them, and re-layouts  2.2 us

profile of v1, /device:TPU:2, one launch (start us, length us, event | category | flops | bytes accessed | tf_op | source)
XLA Modules:
  0.0 60.8 jit_solution(13300935326810453385)
XLA Ops:
  0.6 58.0 %shard_map.86 = (f32[9,4,32,512]{3,2,1,0:T(8,128)S(1)}, f32[2,4,32,512]{3,2,1,0:T(8,128)S(1)}) custom-call(f32[9,4,32,512]{3,2,1,0:T(8,128)} %adj.1, f32[4,32,512]{2,1,0:T(8,128)} %buoy.1, f32[4,32,512]{2,1,0:T(8,128)} %lam.1, f32[4,32,512]{2,1,0:T(8,128)} %shear.1, s32[64,12,2,128]{3,2,1,0:T(2,128)} %bitcast.4, f32[12,1,64]{2,1,0:T(1,128)} %bitcast.5, ...), custom_call_target="tpu_custom_call" | custom-call | tf_op jit(solution)/shard_map/pallas_call | solution.py:546
  58.6 1.4 %copy.11 = f32[9,4,32,512]{3,2,1,0:T(8,128)} copy(f32[9,4,32,512]{3,2,1,0:T(8,128)S(1)} %get-tuple-element.2) | data formatting | bytes 4718592
  60.0 0.8 %copy.12 = f32[2,4,32,512]{3,2,1,0:T(8,128)} copy(f32[2,4,32,512]{3,2,1,0:T(8,128)S(1)} %get-tuple-element.3) | data formatting | bytes 1048576

commit v2 on v1

--- a/solution.py
+++ b/solution.py
@@ -12,12 +12,19 @@
 COURANT = 0.15
 ROWS = 8
 ZBIT = 8
+PAIR = 2
 
 VX, VY, VZ, SXX, SYY, SZZ, SXY, SXZ, SYZ = range(9)
 
-DOWN_S, DOWN_V, DOWN_B, DOWN_C, UP_S, UP_V, UP_B, UP_C = range(8)
-STRESS_Y = ((0, (SYY,), -1), (1, (SXY, SYZ), 1))
-SPEED_Y = ((3, (VX, VZ), -1), (5, (VY,), 1))
+DOWN_S, DOWN_V, DOWN_B, UP_S, UP_V, UP_B = range(6)
+Y_SLOTS = 6
+Y_SYY, Y_SXY, Y_SYZ, Y_VX, Y_VZ, Y_VY = range(Y_SLOTS)
+STRESS_Y = ((Y_SYY, 1, -1), (Y_SXY, 2, 1))
+SPEED_Y = ((Y_VX, 2, -1), (Y_VY, 1, 1))
+BUOY_Y = ((0, 1, -1), (1, 1, 1))
+C_SXY, C_SXZ, C_SYY, C_SXX, C_SYZ = range(5)
+CORNERS = ((1, 1, C_SXY, ((SXY, 1, 1),)), (1, -1, C_SXZ, ((SXZ, 1, 0),)),
+           (-1, -1, C_SYY, ((SYY, 0, 0), (SXX, 0, 0))), (-1, 1, C_SYZ, ((SYZ, 0, 1),)))
 
 
 def partner(me, distance, count):
@@ -32,9 +39,9 @@
 
 
 def kernel(n_x, n_y, adj, buoy, lam, shear, packed, scales, perm, out, grads,
-           cur, coef, strain, halo_x, halo_b, part, corner, corner_send, halo_y, send_y, late_y, late_send,
-           table, scale_v, factor_send, factors, factor_s, perm_v, inv_v, inv,
-           in_sem, xs_sem, xr_sem, ys_sem, yr_sem, ws_sem, wr_sem, fs_sem, fr_sem, loc_sem, *words):
+           cur, coef, strain, halo_x, halo_b, part, corner, corner_send, halo_y, send_y,
+           relay, table, scale_v, factor_send, factors, factor_s, perm_v, inv_v, inv,
+           in_sem, xs_sem, xr_sem, cs_sem, cr_sem, rs_sem, rr_sem, ys_sem, yr_sem, ws_sem, wr_sem, fs_sem, fr_sem, loc_sem, *words):
     cx, cy, cz = buoy.shape
     comp = packed.shape[1]
     per_step = comp // STEPS
@@ -56,6 +63,12 @@
         @pl.when(edge(way, "gy"))
         def _():
             pl.semaphore_signal(barrier, inc=1, device_id={"gy": me_y + way}, device_id_type=MESH)
+
+        for way_x in (-1, 1):
+            @pl.when(edge(way, "gy") & edge(way_x, "gx"))
+            def _():
+                pl.semaphore_signal(barrier, inc=1, device_id={"gx": me_x + way_x, "gy": me_y + way},
+                                    device_id_type=MESH)
 
     loads = {}
     for index in (SXX, SXY, SXZ, SYY, SYZ, SZZ, VX, VY, VZ):
@@ -83,16 +96,12 @@
             src, dst = part.at[step, pl.ds(0, 1)], halo_x.at[step, pl.ds(2, 1)]
         elif kind == DOWN_B:
             src, dst = buoy.at[last], halo_b.at[0]
-        elif kind == DOWN_C:
-            src, dst = corner_send.at[step, pl.ds(0, 1)], corner.at[step, pl.ds(0, 1)]
         elif kind == UP_S:
             src, dst = (adj.at[SXX, 0] if step == 0 else cur.at[SXX, 1]), halo_x.at[step, 3]
         elif kind == UP_V:
             src, dst = part.at[step, pl.ds(1, 2)], halo_x.at[step, pl.ds(4, 2)]
-        elif kind == UP_B:
+        else:
             src, dst = buoy.at[0], halo_b.at[1]
-        else:
-            src, dst = corner_send.at[step, pl.ds(1, 2)], corner.at[step, pl.ds(1, 2)]
         return way, pltpu.make_async_remote_copy(
             src_ref=src, dst_ref=dst, send_sem=xs_sem.at[step, kind], recv_sem=xr_sem.at[step, kind],
             device_id={"gx": me_x + way}, device_id_type=MESH)
@@ -120,33 +129,15 @@
                             copy.wait_send()
 
     def y_copy(step, message):
-        start, fields, way = message
-        slot = 6 * step + start
+        start, count, way = message
+        slot = Y_SLOTS * step + start
         return pltpu.make_async_remote_copy(
-            src_ref=send_y.at[pl.ds(slot, len(fields))], dst_ref=halo_y.at[pl.ds(slot, len(fields))],
+            src_ref=send_y.at[pl.ds(slot, count)], dst_ref=halo_y.at[pl.ds(slot, count)],
             send_sem=ys_sem.at[slot], recv_sem=yr_sem.at[slot],
             device_id={"gy": me_y + way}, device_id_type=MESH)
 
-    def late(step, which):
-        way = -1 if which == 0 else 1
-        first, count = (3 * step, 2) if which == 0 else (3 * step + 2, 1)
-        sem = 6 * STEPS + 2 * step + which
-        return way, pltpu.make_async_remote_copy(
-            src_ref=late_send.at[pl.ds(first, count)], dst_ref=late_y.at[pl.ds(first, count)],
-            send_sem=ys_sem.at[sem], recv_sem=yr_sem.at[sem],
-            device_id={"gy": me_y + way}, device_id_type=MESH)
-
-    def send_rows(step, messages):
-        for message in messages:
-            start, fields, way = message
-
-            @pl.when(edge(way, "gy"))
-            def _():
-                row = 0 if way < 0 else cy - 1
-                for offset, field in enumerate(fields):
-                    for x in range(cx):
-                        send_y[6 * step + start + offset, pl.ds(x, 1), :] = cur[field, 1 + x, pl.ds(row, 1), :]
-                y_copy(step, message).start()
+    def y_start(step, message):
+        y_copy(step, message).start()
 
     def receive_y(step, messages):
         for message in messages:
@@ -154,36 +145,95 @@
             def _():
                 y_copy(step, message).wait_recv()
 
-    def send_late(step):
+    def row_of(field, x, row):
+        return cur[field, 1 + x, pl.ds(row, 1), :]
+
+    def send_buoy_y():
         @pl.when(edge(-1, "gy"))
         def _():
-            late_send[3 * step] = cur[VX, cx, pl.ds(0, 1), :]
-            late_send[3 * step + 1] = cur[VZ, 1, pl.ds(0, 1), :]
-            late(step, 0)[1].start()
+            send_y[Y_SLOTS * STEPS, pl.ds(0, 1), :] = coef[0, last, pl.ds(0, 1), :]
+            send_y[Y_SLOTS * STEPS, pl.ds(1, 1), :] = coef[0, 0, pl.ds(0, 1), :]
+            y_start(STEPS, BUOY_Y[0])
 
         @pl.when(edge(1, "gy"))
         def _():
-            late_send[3 * step + 2] = cur[VY, 1, pl.ds(cy - 1, 1), :]
-            late(step, 1)[1].start()
-
-    def receive_late(step):
+            send_y[Y_SLOTS * STEPS + 1, pl.ds(0, 1), :] = coef[0, 0, pl.ds(cy - 1, 1), :]
+            y_start(STEPS, BUOY_Y[1])
+
+    def send_stress_y(step):
+        slot = Y_SLOTS * step
+
+        @pl.when(edge(-1, "gy"))
+        def _():
+            for x in range(cx):
+                send_y[slot + Y_SYY, pl.ds(x, 1), :] = row_of(SYY, x, 0)
+            y_start(step, STRESS_Y[0])
+
         @pl.when(edge(1, "gy"))
         def _():
-            late(step, 0)[1].wait_recv()
-            halo_y[6 * step + 3, pl.ds(last, 1), :] = late_y[3 * step]
-            halo_y[6 * step + 4, pl.ds(0, 1), :] = late_y[3 * step + 1]
+            for x in range(cx):
+                send_y[slot + Y_SXY, pl.ds(x, 1), :] = row_of(SXY, x, cy - 1)
+                send_y[slot + Y_SYZ, pl.ds(x, 1), :] = row_of(SYZ, x, cy - 1)
+            y_start(step, STRESS_Y[1])
+
+    def send_speed_y(step):
+        slot = Y_SLOTS * step
 
         @pl.when(edge(-1, "gy"))
         def _():
-            late(step, 1)[1].wait_recv()
-            halo_y[6 * step + 5, pl.ds(0, 1), :] = late_y[3 * step + 2]
-
-    def forward_corners(step):
-        slot = 6 * step
-        corner_send[step, 0] = halo_y[slot + 1, pl.ds(last, 1), :]
-        corner_send[step, 1] = halo_y[slot, pl.ds(0, 1), :]
-        corner_send[step, 2] = halo_y[slot + 2, pl.ds(0, 1), :]
-        x_start(step, DOWN_C, UP_C)
+            first = pl.ds(0, 1)
+            for x in range(last):
+                send_y[slot + Y_VX, pl.ds(x, 1), :] = row_of(VX, x, 0)
+                send_y[slot + Y_VZ, pl.ds(x + 1, 1), :] = row_of(VZ, x + 1, 0)
+            send_y[slot + Y_VX, pl.ds(last, 1), :] = part[step, 0, first, :] + (
+                COURANT * coef[0, last, first, :]) * halo_y[slot + Y_SXY, pl.ds(last, 1), :]
+            send_y[slot + Y_VZ, pl.ds(0, 1), :] = part[step, 2, first, :] + (
+                COURANT * coef[0, 0, first, :]) * halo_y[slot + Y_SYZ, pl.ds(0, 1), :]
+            y_start(step, SPEED_Y[0])
+
+        @pl.when(edge(1, "gy"))
+        def _():
+            end = pl.ds(cy - 1, 1)
+            for x in range(1, cx):
+                send_y[slot + Y_VY, pl.ds(x, 1), :] = row_of(VY, x, cy - 1)
+            send_y[slot + Y_VY, pl.ds(0, 1), :] = part[step, 1, end, :] - (
+                COURANT * coef[0, 0, end, :]) * halo_y[slot + Y_SYY, pl.ds(0, 1), :]
+            y_start(step, SPEED_Y[1])
+
+    def fix_rows(step):
+        slot, extra = Y_SLOTS * step, Y_SLOTS * STEPS
+        one, end = pl.ds(0, 1), pl.ds(last, 1)
+        halo_y[slot + Y_VX, end, :] = halo_y[slot + Y_VX, end, :] - (
+            COURANT * halo_y[extra, one, :]) * corner[step, C_SXX]
+        halo_y[slot + Y_VZ, one, :] = halo_y[slot + Y_VZ, one, :] + (
+            COURANT * halo_y[extra, pl.ds(1, 1), :]) * corner[step, C_SXZ]
+        halo_y[slot + Y_VY, one, :] = halo_y[slot + Y_VY, one, :] + (
+            COURANT * halo_y[extra + 1, one, :]) * corner[step, C_SXY]
+
+    def both_edges(way_x, way_y):
+        return edge(way_x, "gx") & edge(way_y, "gy")
+
+    def corner_copy(step, which):
+        way_x, way_y, first, fields = CORNERS[which]
+        slots = pl.ds(first, len(fields))
+        return pltpu.make_async_remote_copy(
+            src_ref=corner_send.at[step, slots], dst_ref=corner.at[step, slots],
+            send_sem=cs_sem.at[step, which], recv_sem=cr_sem.at[step, which],
+            device_id={"gx": me_x + way_x, "gy": me_y + way_y}, device_id_type=MESH)
+
+    def send_corners(step):
+        for which, (way_x, way_y, first, fields) in enumerate(CORNERS):
+            @pl.when(both_edges(way_x, way_y))
+            def _():
+                for offset, (field, layer, row) in enumerate(fields):
+                    corner_send[step, first + offset] = row_of(field, layer * last, row * (cy - 1))
+                corner_copy(step, which).start()
+
+    def receive_corners(step):
+        for which, (way_x, way_y, first, fields) in enumerate(CORNERS):
+            @pl.when(both_edges(-way_x, -way_y))
+            def _():
+                corner_copy(step, which).wait_recv()
 
     def word_copy(distance, step):
         to = partner(me_x, distance, n_x)
@@ -200,6 +250,55 @@
 
     far = [d for d in range(1, n_x) if d & ZBIT]
     near = [d for d in range(1, n_x) if not d & ZBIT]
+
+    outside = ((me_x // 2) % 4 == 0) | ((me_x // 2) % 4 == 3)
+    inside = jnp.logical_not(outside)
+    relayed = [(0, d) for d in far[:16]]
+
+    def relay_in(index):
+        step, distance = relayed[index]
+        to = partner(me_x, distance, n_x)
+        return pltpu.make_async_remote_copy(
+            src_ref=packed.at[to, pl.ds(step * per_step, per_step)], dst_ref=relay.at[index],
+            send_sem=ws_sem.at[distance, step], recv_sem=rr_sem.at[index],
+            device_id={"gx": partner(me_x, PAIR, n_x)}, device_id_type=MESH)
+
+    def relay_out(index):
+        step, distance = relayed[index]
+        return pltpu.make_async_remote_copy(
+            src_ref=relay.at[index], dst_ref=words[step].at[partner(me_x, PAIR, n_x)],
+            send_sem=rs_sem.at[index], recv_sem=wr_sem.at[distance, step],
+            device_id={"gx": partner(me_x, distance ^ PAIR, n_x)}, device_id_type=MESH)
+
+    def send_relays():
+        @pl.when(outside)
+        def _():
+            for index in range(len(relayed)):
+                relay_in(index).start()
+
+    def pass_relays():
+        @pl.when(inside)
+        def _():
+            for index in range(len(relayed)):
+                relay_in(index).wait_recv()
+                relay_out(index).start()
+
+    def finish_relays():
+        @pl.when(inside)
+        def _():
+            for index in range(len(relayed)):
+                relay_out(index).wait_send()
+
+    def words_of(out_words, in_words):
+        @pl.when(outside)
+        def _():
+            for step, distances in out_words:
+                send_words(step, [d for d in distances if (step, d) not in relayed])
+
+        @pl.when(inside)
+        def _():
+            for step, distances in in_words:
+                send_words(step, distances)
 
     def send_words(step, distances):
         for distance in distances:
@@ -262,24 +361,24 @@
                 sxz + (syz - y_before(syz, SYZ, 0, t, None)) + (z_after(szz) - szz))
 
     def velocity(step, which, x, want=(VX, VY, VZ)):
-        slot = 6 * step
+        slot = Y_SLOTS * step
         for t in which:
             rows = pl.ds(t * ROWS, ROWS)
             scaled = COURANT * coef[0, x, rows, :]
             sxy, sxz = tile(SXY, x, t), tile(SXZ, x, t)
             if VX in want:
                 keep(step, VX, x, rows, tile(VX, x, t) - scaled * (
-                    (tile(SXX, x + 1, t) - tile(SXX, x, t)) + (sxy - y_before(sxy, SXY, x, t, slot + 1))
+                    (tile(SXX, x + 1, t) - tile(SXX, x, t)) + (sxy - y_before(sxy, SXY, x, t, slot + Y_SXY))
                     + (sxz - z_before(sxz))))
             if VY in want:
                 syy, syz, szz = tile(SYY, x, t), tile(SYZ, x, t), tile(SZZ, x, t)
                 keep(step, VY, x, rows, tile(VY, x, t) - scaled * (
-                    (sxy - tile(SXY, x - 1, t)) + (y_after(syy, SYY, x, t, slot) - syy) + (syz - z_before(syz))))
+                    (sxy - tile(SXY, x - 1, t)) + (y_after(syy, SYY, x, t, slot + Y_SYY) - syy) + (syz - z_before(syz))))
                 keep(step, VZ, x, rows, tile(VZ, x, t) - scaled * (
-                    (sxz - tile(SXZ, x - 1, t)) + (syz - y_before(syz, SYZ, x, t, slot + 2)) + (z_after(szz) - szz)))
+                    (sxz - tile(SXZ, x - 1, t)) + (syz - y_before(syz, SYZ, x, t, slot + Y_SYZ)) + (z_after(szz) - szz)))
 
     def complete(step):
-        slot = 6 * step
+        slot = Y_SLOTS * step
         for t in range(tiles):
             rows = pl.ds(t * ROWS, ROWS)
 
@@ -289,45 +388,45 @@
             scaled = COURANT * coef[0, last, rows, :]
             more = halo_x[step, 3, rows, :]
             if t == 0:
-                more = edge_row(more, -halo_y[slot + 1, pl.ds(last, 1), :], first_row)
+                more = edge_row(more, -halo_y[slot + Y_SXY, pl.ds(last, 1), :], first_row)
             keep(step, VX, last, rows, part[step, 0, rows, :] - scaled * more)
 
             scaled = COURANT * coef[0, 0, rows, :]
             more = halo_x[step, 0, rows, :]
             if t == tiles - 1:
-                more = edge_row(more, -halo_y[slot, pl.ds(0, 1), :], last_row)
+                more = edge_row(more, -halo_y[slot + Y_SYY, pl.ds(0, 1), :], last_row)
             keep(step, VY, 0, rows, part[step, 1, rows, :] + scaled * more)
             more = halo_x[step, 1, rows, :]
             if t == 0:
-                more = edge_row(more, halo_y[slot + 2, pl.ds(0, 1), :], first_row)
+                more = edge_row(more, halo_y[slot + Y_SYZ, pl.ds(0, 1), :], first_row)
             keep(step, VZ, 0, rows, part[step, 2, rows, :] + scaled * more)
 
             more = tile(SXX, 0, t)
             if t == 0:
-                more = edge_row(more, -corner[step, 0], first_row)
+                more = edge_row(more, -corner[step, C_SXY], first_row)
             cur[VX, 0, rows, :] = halo_x[step, 2, rows, :] - (COURANT * halo_b[0, rows, :]) * more
 
             scaled = COURANT * halo_b[1, rows, :]
             more = tile(SXY, last, t)
             if t == tiles - 1:
-                more = edge_row(more, -corner[step, 1], last_row)
+                more = edge_row(more, -corner[step, C_SYY], last_row)
             cur[VY, cx + 1, rows, :] = halo_x[step, 4, rows, :] + scaled * more
             more = tile(SXZ, last, t)
             if t == 0:
-                more = edge_row(more, corner[step, 2], first_row)
+                more = edge_row(more, corner[step, C_SYZ], first_row)
             cur[VZ, cx + 1, rows, :] = halo_x[step, 5, rows, :] + scaled * more
 
     def stress(step, which, x):
-        slot = 6 * step + 3
+        slot = Y_SLOTS * step
         for t in which:
             rows = pl.ds(t * ROWS, ROWS)
             vx, vy, vz = tile(VX, x, t), tile(VY, x, t), tile(VZ, x, t)
             exx = vx - tile(VX, x - 1, t)
-            eyy = vy - y_before(vy, VY, x, t, slot + 2)
+            eyy = vy - y_before(vy, VY, x, t, slot + Y_VY)
             ezz = vz - z_before(vz)
-            exy = (y_after(vx, VX, x, t, slot) - vx) + (tile(VY, x + 1, t) - vy)
+            exy = (y_after(vx, VX, x, t, slot + Y_VX) - vx) + (tile(VY, x + 1, t) - vy)
             exz = (z_after(vx) - vx) + (tile(VZ, x + 1, t) - vz)
-            eyz = (z_after(vy) - vy) + (y_after(vz, VZ, x, t, slot + 1) - vz)
+            eyz = (z_after(vy) - vy) + (y_after(vz, VZ, x, t, slot + Y_VZ) - vz)
             both = (exx, eyy, ezz, exy, exz, eyz)
             for index, value in enumerate(both):
                 strain[6 * step + index, x, rows, :] = value
@@ -414,6 +513,13 @@
                 grads[0, x, rows, columns] = grad_lambda
                 grads[1, x, rows, columns] = grad_mu
 
+    for way_x, way_y, first, fields in CORNERS:
+        @pl.when(jnp.logical_not(both_edges(-way_x, -way_y)))
+        def _():
+            for step in range(STEPS):
+                for offset in range(len(fields)):
+                    corner[step, first + offset] = jnp.zeros((1, cz), jnp.float32)
+
     for way in (-1, 1):
         @pl.when(jnp.logical_not(edge(way, "gx")))
         def _():
@@ -424,17 +530,15 @@
                 for step in range(STEPS):
                     for slot in (0, 1, 2) if way < 0 else (3, 4, 5):
                         halo_x[step, slot, rows, :] = zero
+
+        @pl.when(jnp.logical_not(edge(way, "gy")))
+        def _():
             for step in range(STEPS):
-                for slot in (0,) if way < 0 else (1, 2):
-                    corner[step, slot] = jnp.zeros((1, cz), jnp.float32)
-
-        @pl.when(jnp.logical_not(edge(way, "gy")))
-        def _():
-            for step in range(STEPS):
-                for start, fields, sent in STRESS_Y + SPEED_Y:
+                for start, count, sent in STRESS_Y + SPEED_Y:
                     if sent == -way:
-                        for offset in range(len(fields)):
-                            halo_y[6 * step + start + offset] = jnp.zeros((cx, cz), jnp.float32)
+                        for offset in range(count):
+                            halo_y[Y_SLOTS * step + start + offset] = jnp.zeros((cx, cz), jnp.float32)
+            halo_y[Y_SLOTS * STEPS + (0 if way > 0 else 1)] = jnp.zeros((cx, cz), jnp.float32)
 
     outer = (0, tiles - 1) if tiles > 1 else (0,)
     inner = range(1, tiles - 1)
@@ -450,10 +554,15 @@
     need(*range(12))
     partials(0)
 
-    pl.semaphore_wait(barrier, n_x - 1 + jnp.minimum(me_y, 1) + jnp.minimum(n_y - 1 - me_y, 1))
-
-    x_start(0, DOWN_S, UP_S, DOWN_V, UP_V, DOWN_B, UP_B)
-    send_rows(0, STRESS_Y)
+    beside_x = jnp.minimum(me_x, 1) + jnp.minimum(n_x - 1 - me_x, 1)
+    beside_y = jnp.minimum(me_y, 1) + jnp.minimum(n_y - 1 - me_y, 1)
+    pl.semaphore_wait(barrier, n_x - 1 + beside_y + beside_x * beside_y)
+
+    send_stress_y(0)
+    send_corners(0)
+    send_buoy_y()
+    x_start(0, DOWN_B, UP_B, DOWN_S, UP_S, DOWN_V, UP_V)
+    send_relays()
     send_words(0, near)
 
     load_scales.wait()
@@ -476,61 +585,76 @@
     own_factor = pltpu.make_async_copy(factor_send.at[me_x], factors.at[me_x], loc_sem.at[1])
     own_factor.start()
 
-    half = len(far) // 2
+    def send_factors():
+        for distance in near + far:
+            factor_copy(distance).start()
+
     for step in range(STEPS):
         if step > 0:
             partials(step)
+            send_stress_y(step)
+            send_corners(step)
             x_start(step, DOWN_S, UP_S, DOWN_V, UP_V)
-            send_rows(step, STRESS_Y)
-            send_words(step, far)
-            send_words(step, near)
+        if step == 1:
+            pass
+            pass
+        velocity(step, inner, 0, (VX,))
+        velocity(step, inner, last, (VY, VZ))
+        over(1, last, functools.partial(velocity, step, inner))
         receive_y(step, STRESS_Y)
-        forward_corners(step)
-        velocity(step, every, 0, (VX,))
-        velocity(step, every, last, (VY, VZ))
-        over(1, last, functools.partial(velocity, step, every))
-        send_rows(step, SPEED_Y)
+        velocity(step, outer, 0, (VX,))
+        velocity(step, outer, last, (VY, VZ))
+        over(1, last, functools.partial(velocity, step, outer))
+        send_speed_y(step)
         if step == 0:
-            send_words(0, far[:half])
-            for distance in near + far:
-                factor_copy(distance).start()
-        receive_y(step, SPEED_Y)
-        over(1, last, functools.partial(stress, step, every))
-        if step > 0:
+            send_factors()
+            pass
+            words_of([(0, far[16:])], [(0, far)])
+        else:
+            pass_relays()
+            words_of([(1, far), (1, near)], [(1, far), (1, near)])
+        over(1, last, functools.partial(stress, step, inner))
+        if step == 1:
             own_factor.wait()
             for distance in near + far:
                 factor_copy(distance).wait()
             to_scalar = pltpu.make_async_copy(factors, factor_s, loc_sem.at[1])
             to_scalar.start()
-            to_scalar.wait()
-            inverse.wait()
-            receive_words(step - 1)
-            over(0, cx, functools.partial(gradient, step - 1))
-        x_wait(step, "recv", DOWN_S, DOWN_V, DOWN_C, UP_S, UP_V, UP_C)
+        x_wait(step, "recv", DOWN_S, DOWN_V, UP_S, UP_V)
         if step == 0:
+            receive_y(STEPS, BUOY_Y)
             x_wait(0, "recv", DOWN_B, UP_B)
+        receive_corners(step)
         complete(step)
-        send_late(step)
+        receive_y(step, SPEED_Y)
         if step == 0:
-            send_words(0, far[half:])
-        ends(functools.partial(stress, step, inner))
-        receive_late(step)
-        ends(functools.partial(stress, step, outer))
+            pass
+            pass
+        fix_rows(step)
+        ends(functools.partial(stress, step, every))
+        over(1, last, functools.partial(stress, step, outer))
+    to_scalar.wait()
+    inverse.wait()
+    receive_words(0)
+    over(0, cx, functools.partial(gradient, 0))
     receive_words(STEPS - 1)
     over(0, cx, functools.partial(gradient, STEPS - 1))
 
+    finish_relays()
     for step in range(STEPS):
-        x_wait(step, "send", DOWN_S, DOWN_V, DOWN_C, UP_S, UP_V, UP_C)
+        x_wait(step, "send", DOWN_S, DOWN_V, UP_S, UP_V)
         for message in STRESS_Y + SPEED_Y:
             @pl.when(edge(message[2], "gy"))
             def _():
                 y_copy(step, message).wait_send()
-        for which in (0, 1):
-            way, copy = late(step, which)
-
-            @pl.when(edge(way, "gy"))
+        for which, (way_x, way_y, _, _) in enumerate(CORNERS):
+            @pl.when(both_edges(way_x, way_y))
             def _():
-                copy.wait_send()
+                corner_copy(step, which).wait_send()
+    for message in BUOY_Y:
+        @pl.when(edge(message[2], "gy"))
+        def _():
+            y_copy(STEPS, message).wait_send()
     x_wait(0, "send", DOWN_B, UP_B)
 
 
@@ -540,7 +664,7 @@
     lanes = min(128, segw)
     packed = packed.reshape(n_x, comp, segw // lanes, lanes)
     scales = jnp.transpose(scales, (0, 3, 2, 1)).reshape(comp, 1, n_x)
-    halos = 6 * STEPS
+    halos = Y_SLOTS * STEPS + 2
     dma = pltpu.SemaphoreType.DMA
     f32, i32 = jnp.float32, jnp.int32
     return pl.pallas_call(
@@ -555,12 +679,11 @@
             pltpu.VMEM((STEPS, 6, cy, cz), f32),
             pltpu.VMEM((2, cy, cz), f32),
             pltpu.VMEM((STEPS, 3, cy, cz), f32),
-            pltpu.VMEM((STEPS, 3, 1, cz), f32),
-            pltpu.VMEM((STEPS, 3, 1, cz), f32),
+            pltpu.VMEM((STEPS, 5, 1, cz), f32),
+            pltpu.VMEM((STEPS, 5, 1, cz), f32),
             pltpu.VMEM((halos, cx, cz), f32),
             pltpu.VMEM((halos, cx, cz), f32),
-            pltpu.VMEM((3 * STEPS, 1, cz), f32),
-            pltpu.VMEM((3 * STEPS, 1, cz), f32),
+            pltpu.VMEM((max(16, 1), comp // STEPS, segw // lanes, lanes), i32),
             pltpu.VMEM((16, 128), f32),
             pltpu.VMEM((comp, 1, n_x), f32),
             pltpu.VMEM((n_x, 1, comp), f32),
@@ -569,7 +692,7 @@
             pltpu.VMEM((1, n_x), i32),
             pltpu.VMEM((1, 128), i32),
             pltpu.SMEM((1, 128), i32),
-            dma((12,)), dma((STEPS, 8)), dma((STEPS, 8)), dma((halos + 2 * STEPS,)), dma((halos + 2 * STEPS,)),
+            dma((12,)), dma((STEPS, 6)), dma((STEPS, 6)), dma((STEPS, 4)), dma((STEPS, 4)), dma((max(16, 1),)), dma((max(16, 1),)), dma((halos,)), dma((halos,)),
             dma((n_x, STEPS)), dma((n_x, STEPS)), dma((n_x,)), dma((n_x,)), dma((2 + STEPS,)),
         ] + [pltpu.VMEM((n_x, comp // STEPS, segw // lanes, lanes), i32)] * STEPS,
         compiler_params=pltpu.CompilerParams(collective_id=0, has_side_effects=True,

time: 60.9 us -> 51.6 us (0.85)
  the two profiles are of different devices: /device:TPU:2 before, /device:TPU:32 now
where the time goes in v2:
time: 51.6 us; the launch traced here: 51.5 us
  Pallas kernels  48.7 us (94%)
  local copies, waits for them, and re-layouts  2.2 us (4%)
  between operations  0.64 us (1%)
    pallas_call x1, Pallas kernels, on_device(): pl.pallas_call(functools.partial(kernel, n_x, n_y), out_shape=(pltpu.VMEM...  48.7 us
    unnamed x2, local copies, waits for them, and re-layouts  2.2 us

profile of v2, /device:TPU:32, one launch (start us, length us, event | category | flops | bytes accessed | tf_op | source)
XLA Modules:
  0.0 51.5 jit_solution(9944816519927663692)
XLA Ops:
  0.6 48.7 %shard_map.86 = (f32[9,4,32,512]{3,2,1,0:T(8,128)S(1)}, f32[2,4,32,512]{3,2,1,0:T(8,128)S(1)}) custom-call(f32[9,4,32,512]{3,2,1,0:T(8,128)} %adj.1, f32[4,32,512]{2,1,0:T(8,128)} %buoy.1, f32[4,32,512]{2,1,0:T(8,128)} %lam.1, f32[4,32,512]{2,1,0:T(8,128)} %shear.1, s32[64,12,2,128]{3,2,1,0:T(2,128)} %bitcast.4, f32[12,1,64]{2,1,0:T(1,128)} %bitcast.5, ...), custom_call_target="tpu_custom_call" | custom-call | tf_op jit(solution)/shard_map/pallas_call | solution.py:670
  49.3 1.4 %copy.11 = f32[9,4,32,512]{3,2,1,0:T(8,128)} copy(f32[9,4,32,512]{3,2,1,0:T(8,128)S(1)} %get-tuple-element.2) | data formatting | bytes 4718592
  50.7 0.8 %copy.12 = f32[2,4,32,512]{3,2,1,0:T(8,128)} copy(f32[2,4,32,512]{3,2,1,0:T(8,128)S(1)} %get-tuple-element.3) | data formatting | bytes 1048576

commit v3 on v2

--- a/solution.py
+++ b/solution.py
@@ -251,9 +251,13 @@
     far = [d for d in range(1, n_x) if d & ZBIT]
     near = [d for d in range(1, n_x) if not d & ZBIT]
 
-    outside = ((me_x // 2) % 4 == 0) | ((me_x // 2) % 4 == 3)
-    inside = jnp.logical_not(outside)
-    relayed = [(0, d) for d in far[:16]]
+    place = me_x % 8
+    slow = (place == 0) | (place == 7)
+    quick = jnp.logical_not(slow)
+    beside = (place == 1) | (place == 6)
+    relays = (place == 2) | (place == 5)
+    inside = (place >= 2) & (place <= 5)
+    relayed = [(0, d) for d in far]
 
     def relay_in(index):
         step, distance = relayed[index]
@@ -271,33 +275,28 @@
             device_id={"gx": partner(me_x, distance ^ PAIR, n_x)}, device_id_type=MESH)
 
     def send_relays():
-        @pl.when(outside)
+        @pl.when(slow)
         def _():
             for index in range(len(relayed)):
                 relay_in(index).start()
 
     def pass_relays():
-        @pl.when(inside)
+        @pl.when(relays)
         def _():
             for index in range(len(relayed)):
                 relay_in(index).wait_recv()
                 relay_out(index).start()
 
     def finish_relays():
-        @pl.when(inside)
+        @pl.when(relays)
         def _():
             for index in range(len(relayed)):
                 relay_out(index).wait_send()
 
-    def words_of(out_words, in_words):
-        @pl.when(outside)
-        def _():
-            for step, distances in out_words:
-                send_words(step, [d for d in distances if (step, d) not in relayed])
-
-        @pl.when(inside)
-        def _():
-            for step, distances in in_words:
+    def words_of(where, *which):
+        @pl.when(where)
+        def _():
+            for step, distances in which:
                 send_words(step, distances)
 
     def send_words(step, distances):
@@ -597,7 +596,7 @@
             x_start(step, DOWN_S, UP_S, DOWN_V, UP_V)
         if step == 1:
             pass
-            pass
+            words_of(beside, (1, far))
         velocity(step, inner, 0, (VX,))
         velocity(step, inner, last, (VY, VZ))
         over(1, last, functools.partial(velocity, step, inner))
@@ -609,10 +608,11 @@
         if step == 0:
             send_factors()
             pass
-            words_of([(0, far[16:])], [(0, far)])
+            words_of(quick, (0, far))
         else:
             pass_relays()
-            words_of([(1, far), (1, near)], [(1, far), (1, near)])
+            words_of(jnp.logical_not(beside), (1, far))
+            send_words(1, near)
         over(1, last, functools.partial(stress, step, inner))
         if step == 1:
             own_factor.wait()
@@ -683,7 +683,7 @@
             pltpu.VMEM((STEPS, 5, 1, cz), f32),
             pltpu.VMEM((halos, cx, cz), f32),
             pltpu.VMEM((halos, cx, cz), f32),
-            pltpu.VMEM((max(16, 1), comp // STEPS, segw // lanes, lanes), i32),
+            pltpu.VMEM((max(32, 1), comp // STEPS, segw // lanes, lanes), i32),
             pltpu.VMEM((16, 128), f32),
             pltpu.VMEM((comp, 1, n_x), f32),
             pltpu.VMEM((n_x, 1, comp), f32),
@@ -692,7 +692,7 @@
             pltpu.VMEM((1, n_x), i32),
             pltpu.VMEM((1, 128), i32),
             pltpu.SMEM((1, 128), i32),
-            dma((12,)), dma((STEPS, 6)), dma((STEPS, 6)), dma((STEPS, 4)), dma((STEPS, 4)), dma((max(16, 1),)), dma((max(16, 1),)), dma((halos,)), dma((halos,)),
+            dma((12,)), dma((STEPS, 6)), dma((STEPS, 6)), dma((STEPS, 4)), dma((STEPS, 4)), dma((max(32, 1),)), dma((max(32, 1),)), dma((halos,)), dma((halos,)),
             dma((n_x, STEPS)), dma((n_x, STEPS)), dma((n_x,)), dma((n_x,)), dma((2 + STEPS,)),
         ] + [pltpu.VMEM((n_x, comp // STEPS, segw // lanes, lanes), i32)] * STEPS,
         compiler_params=pltpu.CompilerParams(collective_id=0, has_side_effects=True,

time: 51.6 us -> 51.5 us (level)
  the two profiles are of different devices: /device:TPU:32 before, /device:TPU:38 now
where the time goes in v3:
time: 51.5 us; the launch traced here: 51.4 us
  Pallas kernels  48.6 us (94%)
  local copies, waits for them, and re-layouts  2.2 us (4%)
  between operations  0.64 us (1%)
    pallas_call x1, Pallas kernels, on_device(): pl.pallas_call(functools.partial(kernel, n_x, n_y), out_shape=(pltpu.VMEM...  48.6 us
    unnamed x2, local copies, waits for them, and re-layouts  2.2 us

profile of v3, /device:TPU:38, one launch (start us, length us, event | category | flops | bytes accessed | tf_op | source)
XLA Modules:
  0.0 51.4 jit_solution(3763646744356073891)
XLA Ops:
  0.6 48.6 %shard_map.86 = (f32[9,4,32,512]{3,2,1,0:T(8,128)S(1)}, f32[2,4,32,512]{3,2,1,0:T(8,128)S(1)}) custom-call(f32[9,4,32,512]{3,2,1,0:T(8,128)} %adj.1, f32[4,32,512]{2,1,0:T(8,128)} %buoy.1, f32[4,32,512]{2,1,0:T(8,128)} %lam.1, f32[4,32,512]{2,1,0:T(8,128)} %shear.1, s32[64,12,2,128]{3,2,1,0:T(2,128)} %bitcast.4, f32[12,1,64]{2,1,0:T(1,128)} %bitcast.5, ...), custom_call_target="tpu_custom_call" | custom-call | tf_op jit(solution)/shard_map/pallas_call | solution.py:670
  49.2 1.4 %copy.11 = f32[9,4,32,512]{3,2,1,0:T(8,128)} copy(f32[9,4,32,512]{3,2,1,0:T(8,128)S(1)} %get-tuple-element.2) | data formatting | bytes 4718592
  50.6 0.8 %copy.12 = f32[2,4,32,512]{3,2,1,0:T(8,128)} copy(f32[2,4,32,512]{3,2,1,0:T(8,128)S(1)} %get-tuple-element.3) | data formatting | bytes 1048576
